TPU v7x, 32 devices: a whole 2x2x4 slice. The times are simulated.
32 devices in a mesh: blk: 32 (over z, y, x, core).
Axes of the slice: x: 2, y: 2, z: 4, core: 2. Of those that a mesh axis runs over, the one named last changes fastest.
Arguments:
- image_features: bfloat16 [8192, 1536], P('blk'), may hold values from -0.119628906 to 0.119628906
- head_weight: bfloat16 [1536, 1152], P('blk'), may hold values from -0.15625 to 0.15625
- text_embeds: bfloat16 [8192, 1152], P('blk'), may hold values from -0.29882812 to 0.29882812
- natural_exponent_factor: float32 [1], replicated, may hold values from 1.6 to 2.6
- logit_bias: float32 [1], replicated, may hold values from -4 to -1
Outputs:
- grad_features: bfloat16 [8192, 1536], P('blk')
- grad_text: bfloat16 [8192, 1152], P('blk')
- grad_weight: float32 [1536, 1152], P('blk')
All inputs are finite; a program needn't handle non-finite values.
Results may differ from a plain program's by a relative error of at most 0.0085.
Values may be sent and summed in bfloat16 or wider, within the bound.
A program may use at most 64 MiB of HBM per device.

v0:
```python
import jax
import jax.numpy as jnp
from jax import lax
from jax.sharding import PartitionSpec as P

S = 4


epsilon = 1e-06


def passed_along(block, axis, distance):
    devices = range(lax.axis_size(axis))
    route = [((i - distance) % len(devices), i) for i in devices]
    return lax.ppermute(block, axis, route)


def normalize(rows):
    squares = jnp.sum(rows * rows, axis=1, keepdims=True)
    length = jnp.sqrt(squares + epsilon)
    return (rows / length, length)


def similarity_derivative(
    picture_sample_group,
    caption_sample_group,
    similarity_multiplier,
    neighbour_distance,
    outer_dimension_size,
):
    similarity_matrix = (
        similarity_multiplier
        * lax.dot_general(
            picture_sample_group,
            caption_sample_group,
            (((1,), (1,)), ((), ())),
            preferred_element_type=jnp.float32,
        )
        + neighbour_distance
    )
    if outer_dimension_size:
        matched = lax.broadcasted_iota(
            jnp.int32, similarity_matrix.shape, 0
        ) == lax.broadcasted_iota(jnp.int32, similarity_matrix.shape, 1)
        match_polarity = jnp.where(matched, 1.0, -1.0).astype(jnp.float32)
    else:
        match_polarity = -jnp.ones(similarity_matrix.shape, jnp.float32)
    return (
        -similarity_multiplier
        * match_polarity
        * jax.nn.sigmoid(-match_polarity * similarity_matrix)
    ).astype(jnp.bfloat16)


def project_back(grad, unit_rows, length):
    return (grad - unit_rows * jnp.sum(unit_rows * grad, axis=1, keepdims=True)) / length


def on_device(image_features, head_weight, text_embeds, natural_exponent_factor, logit_bias):
    full_weight = lax.all_gather(head_weight, "blk", axis=0, tiled=True)
    embedded = jnp.dot(image_features, full_weight, preferred_element_type=jnp.float32)
    image_unit, image_length = normalize(embedded)
    picture_embedding_mapped = image_unit.astype(jnp.bfloat16)
    text_unit, text_length = normalize(text_embeds.astype(jnp.float32))
    text_low = text_unit.astype(jnp.bfloat16)
    similarity_multiplier = jnp.exp(natural_exponent_factor[0])
    neighbour_distance = logit_bias[0]
    image_grad = jnp.zeros(image_unit.shape, jnp.float32)
    current_neighbour_tile = text_low
    for partition_portion in range(S):
        mapping_matrix = similarity_derivative(
            picture_embedding_mapped,
            current_neighbour_tile,
            similarity_multiplier,
            neighbour_distance,
            partition_portion == 0,
        )
        image_grad = image_grad + jnp.dot(
            mapping_matrix, current_neighbour_tile, preferred_element_type=jnp.float32
        )
        if partition_portion + 1 < S:
            current_neighbour_tile = passed_along(current_neighbour_tile, "blk", -1)
    text_grad = jnp.zeros(text_unit.shape, jnp.float32)
    passing = picture_embedding_mapped
    for partition_portion in range(S):
        mapping_matrix = similarity_derivative(
            passing, text_low, similarity_multiplier, neighbour_distance, partition_portion == 0
        )
        text_grad = text_grad + lax.dot_general(
            mapping_matrix, passing, (((0,), (0,)), ((), ())), preferred_element_type=jnp.float32
        )
        if partition_portion + 1 < S:
            passing = passed_along(passing, "blk", 1)
    embed_grad = project_back(image_grad, image_unit, image_length).astype(jnp.bfloat16)
    grad_text = project_back(text_grad, text_unit, text_length).astype(jnp.bfloat16)
    grad_features = lax.dot_general(
        embed_grad, full_weight, (((1,), (1,)), ((), ())), preferred_element_type=jnp.float32
    ).astype(jnp.bfloat16)
    grad_weight = lax.psum_scatter(
        lax.dot_general(
            image_features, embed_grad, (((0,), (0,)), ((), ())), preferred_element_type=jnp.float32
        ),
        "blk",
        scatter_dimension=0,
        tiled=True,
    )
    return (grad_features, grad_text, grad_weight)


def solution(mesh):
    return jax.shard_map(
        on_device,
        mesh=mesh,
        in_specs=(P("blk", None), P("blk", None), P("blk", None), P(), P()),
        out_specs=(P("blk", None), P("blk", None), P("blk", None)),
        check_vma=False,
    )
```

profile of v0, /device:TPU:0, one launch (start us, length us, event | category | flops | bytes accessed | tf_op | source)
XLA Modules:
  0.0 235.9 jit_solution(13343225340845316191)
XLA Ops:
  7.2 0.0 all-gather.2.cloned.1.call-start
  7.2 0.7 all-gather.2.cloned.1.call-update
  7.9 0.0 reduce-scatter.4.cloned.1.call-start
  8.0 1.3 fusion
  9.2 1.3 fusion.81
  10.5 6.5 %collective-permute-start = (bf16[256,1152]{1,0:T(8,128)(2,1)S(1)}, bf16[256,1152]{1,0:T(8,128)(2,1)S(1)}, u32[]{:S(2)}, u32[]{:S(2)}) collective-permute-start(bf16[256,1152]{1,0:T(8,128)(2,1)S(1)} %fusion.81), channel_id=1, source_target_pairs={{1,0},{2,1},{3,2},{4,3},{5,4},{6,5},{7,6},{8,7},{9,8},{10,9},{11,1... | collective-permute-start | bytes 1769480 | tf_op jit(solution)/shard_map/ppermute | solution.py:15
  17.0 8.2 %collective-permute-done = bf16[256,1152]{1,0:T(8,128)(2,1)S(1)} collective-permute-done((bf16[256,1152]{1,0:T(8,128)(2,1)S(1)}, bf16[256,1152]{1,0:T(8,128)(2,1)S(1)}, u32[]{:S(2)}, u32[]{:S(2)}) %collective-permute-start) | collective-permute-done | bytes 589856 | tf_op jit(solution)/shard_map/ppermute | solution.py:15
  25.2 5.5 %collective-permute-start.1 = (bf16[256,1152]{1,0:T(8,128)(2,1)S(1)}, bf16[256,1152]{1,0:T(8,128)(2,1)}, u32[]{:S(2)}, u32[]{:S(2)}) collective-permute-start(bf16[256,1152]{1,0:T(8,128)(2,1)S(1)} %collective-permute-done), channel_id=1, source_target_pairs={{1,0},{2,1},{3,2},{4,3},{5,4},{6,5},{7,6},{8,7},{9,8},{10,9},{11,1... | collective-permute-start | bytes 1769480 | tf_op jit(solution)/shard_map/ppermute | solution.py:15
  32.0 6.2 %collective-permute-done.1 = bf16[256,1152]{1,0:T(8,128)(2,1)} collective-permute-done((bf16[256,1152]{1,0:T(8,128)(2,1)S(1)}, bf16[256,1152]{1,0:T(8,128)(2,1)}, u32[]{:S(2)}, u32[]{:S(2)}) %collective-permute-start.1) | collective-permute-done | bytes 589856 | tf_op jit(solution)/shard_map/ppermute | solution.py:15
  38.2 5.7 %collective-permute-start.2 = (bf16[256,1152]{1,0:T(8,128)(2,1)}, bf16[256,1152]{1,0:T(8,128)(2,1)}, u32[]{:S(2)}, u32[]{:S(2)}) collective-permute-start(bf16[256,1152]{1,0:T(8,128)(2,1)} %collective-permute-done.1), channel_id=1, source_target_pairs={{1,0},{2,1},{3,2},{4,3},{5,4},{6,5},{7,6},{8,7},{9,8},{10,9},{11,1... | collective-permute-start | bytes 1769480 | tf_op jit(solution)/shard_map/ppermute | solution.py:15
  43.9 37.6 %all-gather.2.cloned.1.call-done = bf16[1536,1152]{1,0:T(8,128)(2,1)} async-done(((bf16[48,1152]{1,0:T(8,128)(2,1)}), bf16[1536,1152]{1,0:T(8,128)(2,1)}) %all-gather.2.cloned.1.call-update) | async-done | bytes 3538960 | tf_op jit(solution)/shard_map/all_gather | solution.py:60
  81.5 3.3 %multiply_reduce_fusion.2 = (f32[256]{0:T(256)S(1)}, f32[256,1152]{1,0:T(8,128)S(1)}) fusion(bf16[256,1536]{1,0:T(8,128)(2,1)S(1)} %copy-done, bf16[1536,1152]{1,0:T(8,128)(2,1)} %all-gather.2.cloned.1.call-done), kind=kOutput, calls=%fused_computation.15 | convolution fusion | flops 906559232 | bytes 5506048 | tf_op jit(solution)/shard_map/dot_general | solution.py:61
  84.8 0.1 fusion.82
  85.0 0.4 fusion.44
  85.4 0.4 copy-done.4
  85.8 1.4 fusion.83
  87.2 2.6 %convolution_add_fusion.5 = f32[256,1152]{1,0:T(8,128)S(1)} fusion(f32[256,1152]{1,0:T(8,128)} %fusion.83, bf16[256,1152]{1,0:T(8,128)(2,1)} %copy-done.2, bf16[256,1152]{1,0:T(8,128)(2,1)S(1)} %fusion.82, f32[]{:T(128)S(6)} %mul.119, f32[]{:T(128)} %bitcast.39, f32[]{:T(128)} %bitcast), kind=kOutput, calls=%fused_computation.6 | convolution fusion | flops 302743552 | bytes 3538956 | tf_op jit(solution)/shard_map/dot_general | solution.py:78
  89.7 3.2 %convolution_add_fusion.4 = f32[256,1152]{1,0:T(8,128)} fusion(f32[256,1152]{1,0:T(8,128)S(1)} %convolution_add_fusion.5, bf16[256,1152]{1,0:T(8,128)(2,1)} %collective-permute-done.1, bf16[256,1152]{1,0:T(8,128)(2,1)S(1)} %fusion.82, f32[]{:T(128)S(6)} %mul.119, f32[]{:T(128)} %bitcast.38, f32[]{:T(128)} %bitcast), kind=kOutput, calls=%fused_computation.5 | convolution fusion | flops 302743552 | bytes 3538956 | tf_op jit(solution)/shard_map/dot_general | solution.py:78
  93.0 4.1 %multiply_reduce_fusion.1 = (f32[256]{0:T(256)S(1)}, f32[256,1152]{1,0:T(8,128)}) fusion(f32[256,1152]{1,0:T(8,128)} %copy-done.4, f32[256]{0:T(256)S(1)} %add_sqrt_fusion.1, f32[256,1152]{1,0:T(8,128)} %convolution_add_fusion.4, bf16[256,1152]{1,0:T(8,128)(2,1)} %collective-permute-done.2, bf16[256,1152]{1,0:T(8,128)(2,1)S(1)} %fusion.82, f32[]{:T(128)S(6)} %mul.119, ...), kind=kOutput, calls=%fused_computation.14 | convolution fusion | flops 303628032 | bytes 4720652 | tf_op jit(solution)/shard_map/dot_general | solution.py:78
  97.1 5.5 %convolution_bitcast_fusion = f32[1536,1152]{0,1:T(8,128)} fusion(bf16[256,1536]{1,0:T(8,128)(2,1)S(1)} %copy-done, f32[256,1152]{1,0:T(8,128)} %get-tuple-element.12, f32[256]{0:T(256)S(1)} %get-tuple-element.11, f32[256]{0:T(256)S(1)} %add_sqrt_fusion.1, f32[256,1152]{1,0:T(8,128)S(1)} %copy-done.5), kind=kOutput, calls=%fused_computation | convolution fusion | flops 907444224 | bytes 10225664 | tf_op jit(solution)/shard_map/dot_general | solution.py:100
  102.6 8.1 %copy.10 = f32[1536,1152]{1,0:T(8,128)} copy(f32[1536,1152]{0,1:T(8,128)} %convolution_bitcast_fusion) | data formatting | bytes 14155776
  110.7 0.3 collective-permute-start.3
  111.0 1.4 fusion.84
  112.3 11.3 %collective-permute-done.3 = bf16[256,1152]{1,0:T(8,128)(2,1)S(1)} collective-permute-done((bf16[256,1152]{1,0:T(8,128)(2,1)S(1)}, bf16[256,1152]{1,0:T(8,128)(2,1)S(1)}, u32[]{:S(2)}, u32[]{:S(2)}) %collective-permute-start.3) | collective-permute-done | bytes 589856 | tf_op jit(solution)/shard_map/ppermute | solution.py:15
  123.6 4.5 %convolution_convert_fusion = bf16[256,1536]{1,0:T(8,128)(2,1)} fusion(bf16[1536,1152]{1,0:T(8,128)(2,1)} %all-gather.2.cloned.1.call-done, f32[256,1152]{1,0:T(8,128)S(1)} %copy-done.6, f32[256]{0:T(256)S(1)} %get-tuple-element.11, f32[256]{0:T(256)S(1)} %add_sqrt_fusion.1, f32[256,1152]{1,0:T(8,128)S(1)} %copy-done.5), kind=kOutput, calls=%fused_computation.7 | convolution fusion | flops 907837440 | bytes 6686720 | tf_op jit(solution)/shard_map/dot_general | solution.py:96
  128.1 8.5 %collective-permute-done.4 = bf16[256,1152]{1,0:T(8,128)(2,1)} collective-permute-done((bf16[256,1152]{1,0:T(8,128)(2,1)S(1)}, bf16[256,1152]{1,0:T(8,128)(2,1)}, u32[]{:S(2)}, u32[]{:S(2)}) %collective-permute-start.4) | collective-permute-done | bytes 589856 | tf_op jit(solution)/shard_map/ppermute | solution.py:15
  136.6 2.8 %convolution_add_fusion.2 = f32[256,1152]{1,0:T(8,128)S(1)} fusion(f32[256,1152]{1,0:T(8,128)} %fusion.84, bf16[256,1152]{1,0:T(8,128)(2,1)} %copy-done.3, bf16[256,1152]{1,0:T(8,128)(2,1)S(1)} %fusion.81, f32[]{:T(128)S(6)} %mul.119, f32[]{:T(128)} %bitcast.36, f32[]{:T(128)} %bitcast), kind=kOutput, calls=%fused_computation.3 | convolution fusion | flops 302743552 | bytes 3538956 | tf_op jit(solution)/shard_map/dot_general | solution.py:89
  139.4 3.4 %convolution_add_fusion.1 = f32[256,1152]{1,0:T(8,128)} fusion(f32[256,1152]{1,0:T(8,128)S(1)} %convolution_add_fusion.2, bf16[256,1152]{1,0:T(8,128)(2,1)} %collective-permute-done.4, bf16[256,1152]{1,0:T(8,128)(2,1)S(1)} %fusion.81, f32[]{:T(128)S(6)} %mul.119, f32[]{:T(128)} %bitcast.35, f32[]{:T(128)} %bitcast), kind=kOutput, calls=%fused_computation.2 | convolution fusion | flops 302743552 | bytes 3538956 | tf_op jit(solution)/shard_map/dot_general | solution.py:89
  142.8 7.0 %collective-permute-done.5 = bf16[256,1152]{1,0:T(8,128)(2,1)} collective-permute-done((bf16[256,1152]{1,0:T(8,128)(2,1)}, bf16[256,1152]{1,0:T(8,128)(2,1)}, u32[]{:S(2)}, u32[]{:S(2)}) %collective-permute-start.5) | collective-permute-done | bytes 589856 | tf_op jit(solution)/shard_map/ppermute | solution.py:15
  149.8 2.8 %multiply_reduce_fusion = (f32[256]{0:T(256)S(1)}, f32[256,1152]{1,0:T(8,128)S(1)}) fusion(f32[256]{0:T(256)S(1)} %add_sqrt_fusion, bf16[256,1152]{1,0:T(8,128)(2,1)S(1)} %copy-done.1, f32[256,1152]{1,0:T(8,128)} %convolution_add_fusion.1, bf16[256,1152]{1,0:T(8,128)(2,1)} %collective-permute-done.5, bf16[256,1152]{1,0:T(8,128)(2,1)S(1)} %fusion.81, ...), kind=kOutput, calls=%fused_computation.12 | convolution fusion | flops 303922944 | bytes 4130828 | tf_op jit(solution)/shard_map/dot_general | solution.py:89
  152.6 1.1 divide_convert_fusion
  153.7 75.3 %reduce-scatter.4.cloned.1.call-done = f32[48,1152]{1,0:T(8,128)} async-done(((f32[1536,1152]{1,0:T(8,128)}), f32[48,1152]{1,0:T(8,128)}) %reduce-scatter.4.cloned.1.call-update) | async-done | bytes 221200
  (19 shorter events, 0.1 us)
Async XLA Ops:
  7.2 74.3 %copy-start = (bf16[256,1536]{1,0:T(8,128)(2,1)S(1)}, bf16[256,1536]{1,0:T(8,128)(2,1)}, u32[]{:S(2)}) copy-start(bf16[256,1536]{1,0:T(8,128)(2,1)} %param.5) | copy-start | bytes 2359300
  7.2 74.3 %all-gather.2.cloned.1.call-start = ((), (), s32[]{:S(2)}) async-start(), calls=%async_computation.1 | async-start | bytes 3649536 | tf_op jit(solution)/shard_map/all_gather | solution.py:60
  7.9 221.2 %reduce-scatter.4.cloned.1.call-start = ((), (), s32[]{:S(2)}) async-start(), calls=%async_computation.2 | async-start | bytes 7299072
  10.5 14.6 %collective-permute-start = (bf16[256,1152]{1,0:T(8,128)(2,1)S(1)}, bf16[256,1152]{1,0:T(8,128)(2,1)S(1)}, u32[]{:S(2)}, u32[]{:S(2)}) collective-permute-start(bf16[256,1152]{1,0:T(8,128)(2,1)S(1)} %fusion.81), channel_id=1, source_target_pairs={{1,0},{2,1},{3,2},{4,3},{5,4},{6,5},{7,6},{8,7},{9,8},{10,9},{11,1... | collective-permute-start | bytes 1769480 | tf_op jit(solution)/shard_map/ppermute | solution.py:15
  25.2 59.6 %copy-start.2 = (bf16[256,1152]{1,0:T(8,128)(2,1)}, bf16[256,1152]{1,0:T(8,128)(2,1)S(1)}, u32[]{:S(2)}) copy-start(bf16[256,1152]{1,0:T(8,128)(2,1)S(1)} %collective-permute-done) | copy-start | bytes 1769476
  25.2 13.1 %collective-permute-start.1 = (bf16[256,1152]{1,0:T(8,128)(2,1)S(1)}, bf16[256,1152]{1,0:T(8,128)(2,1)}, u32[]{:S(2)}, u32[]{:S(2)}) collective-permute-start(bf16[256,1152]{1,0:T(8,128)(2,1)S(1)} %collective-permute-done), channel_id=1, source_target_pairs={{1,0},{2,1},{3,2},{4,3},{5,4},{6,5},{7,6},{8,7},{9,8},{10,9},{11,1... | collective-permute-start | bytes 1769480 | tf_op jit(solution)/shard_map/ppermute | solution.py:15
  38.2 54.7 %collective-permute-start.2 = (bf16[256,1152]{1,0:T(8,128)(2,1)}, bf16[256,1152]{1,0:T(8,128)(2,1)}, u32[]{:S(2)}, u32[]{:S(2)}) collective-permute-start(bf16[256,1152]{1,0:T(8,128)(2,1)} %collective-permute-done.1), channel_id=1, source_target_pairs={{1,0},{2,1},{3,2},{4,3},{5,4},{6,5},{7,6},{8,7},{9,8},{10,9},{11,1... | collective-permute-start | bytes 1769480 | tf_op jit(solution)/shard_map/ppermute | solution.py:15
  84.8 1.0 copy-start.4
  93.0 4.1 %copy-start.5 = (f32[256,1152]{1,0:T(8,128)S(1)}, f32[256,1152]{1,0:T(8,128)}, u32[]{:S(2)}) copy-start(f32[256,1152]{1,0:T(8,128)} %copy-done.4) | copy-start | bytes 3538948
  110.6 13.0 %copy-start.6 = (f32[256,1152]{1,0:T(8,128)S(1)}, f32[256,1152]{1,0:T(8,128)}, u32[]{:S(2)}) copy-start(f32[256,1152]{1,0:T(8,128)} %get-tuple-element.12) | copy-start | bytes 3538948
  110.7 13.0 %collective-permute-start.3 = (bf16[256,1152]{1,0:T(8,128)(2,1)S(1)}, bf16[256,1152]{1,0:T(8,128)(2,1)S(1)}, u32[]{:S(2)}, u32[]{:S(2)}) collective-permute-start(bf16[256,1152]{1,0:T(8,128)(2,1)S(1)} %fusion.82), channel_id=1, source_target_pairs={{31,0},{0,1},{1,2},{2,3},{3,4},{4,5},{5,6},{6,7},{7,8},{8,9},{9,10... | collective-permute-start | bytes 1769480 | tf_op jit(solution)/shard_map/ppermute | solution.py:15
  123.6 4.5 %copy-start.3 = (bf16[256,1152]{1,0:T(8,128)(2,1)}, bf16[256,1152]{1,0:T(8,128)(2,1)S(1)}, u32[]{:S(2)}) copy-start(bf16[256,1152]{1,0:T(8,128)(2,1)S(1)} %collective-permute-done.3) | copy-start | bytes 1769476
  123.6 13.0 %collective-permute-start.4 = (bf16[256,1152]{1,0:T(8,128)(2,1)S(1)}, bf16[256,1152]{1,0:T(8,128)(2,1)}, u32[]{:S(2)}, u32[]{:S(2)}) collective-permute-start(bf16[256,1152]{1,0:T(8,128)(2,1)S(1)} %collective-permute-done.3), channel_id=1, source_target_pairs={{31,0},{0,1},{1,2},{2,3},{3,4},{4,5},{5,6},{6,7},{7,8},{8,9},{9,10... | collective-permute-start | bytes 1769480 | tf_op jit(solution)/shard_map/ppermute | solution.py:15
  136.6 13.2 %collective-permute-start.5 = (bf16[256,1152]{1,0:T(8,128)(2,1)}, bf16[256,1152]{1,0:T(8,128)(2,1)}, u32[]{:S(2)}, u32[]{:S(2)}) collective-permute-start(bf16[256,1152]{1,0:T(8,128)(2,1)} %collective-permute-done.4), channel_id=1, source_target_pairs={{31,0},{0,1},{1,2},{2,3},{3,4},{4,5},{5,6},{6,7},{7,8},{8,9},{9,10... | collective-permute-start | bytes 1769480 | tf_op jit(solution)/shard_map/ppermute | solution.py:15
  139.4 10.5 %copy-start.1 = (bf16[256,1152]{1,0:T(8,128)(2,1)S(1)}, bf16[256,1152]{1,0:T(8,128)(2,1)}, u32[]{:S(2)}) copy-start(bf16[256,1152]{1,0:T(8,128)(2,1)} %param.7) | copy-start | bytes 1769476
Sparse Core Ops, SparseCore 0:
  10.9 70.5 all-gather.1
  110.8 118.2 reduce-scatter.3
where the time goes:
time: 236 us
  waiting for transfers between devices  155 us (66%)
  matrix products  35.2 us (15%)
  starting transfers between devices  18 us (8%)
  between operations  15.5 us (7%)
  local copies, waits for them, and re-layouts  8.52 us (4%)
  other arithmetic  3.83 us (2%)
    unnamed x3, waiting for transfers between devices  76 us
    ppermute x6, waiting for transfers between devices, passed_along(): return lax.ppermute(block, axis, route)  41.2 us
    all_gather x1, waiting for transfers between devices, on_device(): full_weight = lax.all_gather(head_weight, 'blk', axis=0, tiled=True)  37.6 us
    ppermute x6, starting transfers between devices, passed_along(): return lax.ppermute(block, axis, route)  17.9 us
    dot_general x4, matrix products, on_device(): jnp.dot(mapping_matrix, current_neighbour_tile, preferred_element_type=jn...  11.3 us
    dot_general x4, matrix products, on_device(): lax.dot_general(mapping_matrix, passing, (((0,), (0,)), ((), ())), prefer...  10.3 us
    unnamed x15, local copies, waits for them, and re-layouts  8.52 us
    dot_general x1, matrix products, on_device(): lax.dot_general(image_features, embed_grad, (((0,), (0,)), ((), ())), pre...  5.49 us
  transfers between devices with their start and end apart: 8, of which 7 were waited for; matrix products, arithmetic and copies ran while one was open for 12% of the time, Pallas kernels for 0%

commit v1 on v0

--- a/solution.py
+++ b/solution.py
@@ -1,12 +1,339 @@
+import functools
+
 import jax
 import jax.numpy as jnp
 from jax import lax
+from jax.experimental import pallas as pl
+from jax.experimental.pallas import tpu as pltpu
 from jax.sharding import PartitionSpec as P
 
 S = 4
-
-
 epsilon = 1e-06
+MESH = pl.DeviceIdType.MESH
+F32 = jnp.float32
+BF = jnp.bfloat16
+
+
+def dot_nt(a, b):
+    return lax.dot_general(a, b, (((1,), (1,)), ((), ())), preferred_element_type=F32)
+
+
+def pair_grad(rows, cols, t, bias, own):
+    logits = t * dot_nt(rows, cols) + bias
+    if own:
+        matched = lax.broadcasted_iota(jnp.int32, logits.shape, 0) == lax.broadcasted_iota(
+            jnp.int32, logits.shape, 1
+        )
+        z = jnp.where(matched, 1.0, -1.0).astype(F32)
+        return (-t * z * jax.nn.sigmoid(-z * logits)).astype(BF)
+    return (t * jax.nn.sigmoid(logits)).astype(BF)
+
+
+def sem_keys(depth):
+    keys = [("z", d) for d in range(1, depth)]
+    for d in range(depth):
+        keys += [("x1", d), ("y1", d), ("y3", d, 0), ("y3", d, 1), ("x3", d, 0), ("x3", d, 1)]
+        keys += [("w", d, i) for i in range(7)]
+        keys += [(k, d) for k in ("g0", "g1a", "g1b", "g2a", "g2b", "g3")]
+    for k in ("t", "i"):
+        keys += [(k, "in", 0), (k, "in", 1), (k, "on", 0), (k, "on", 1), (k, "far")]
+    return {k: i for i, k in enumerate(keys)}
+
+
+def kernel(
+    n, axis, keys,
+    x_ref, w_ref, t_ref, lf_ref, bias_ref,
+    gx_ref, gt_ref, gw_ref,
+    w_all, text_low, text_in, image_low, image_in, xt, gz, from_core, to_core,
+    s1a, s1b, r1a, r1b, s2a, s2b, r2a, r2b, s3, r3,
+    send_sem, recv_sem,
+):
+    depth = n // 8
+    rows, width = x_ref.shape
+    own_rows, cols = w_ref.shape
+    half = rows // 2
+    ha = (cols // 128 + 1) // 2 * 128
+    A, B = pl.ds(0, ha), pl.ds(ha, cols - ha)
+    me = lax.axis_index(axis)
+    core = lax.rem(me, 2)
+    chip = me // 2
+    x = lax.rem(chip, 2)
+    y = lax.rem(chip // 2, 2)
+    z = chip // 4
+
+    def dev(z_, y_, x_, c_):
+        return ((z_ * 2 + y_) * 2 + x_) * 2 + c_
+
+    def up(d):
+        return lax.rem(z + d, depth)
+
+    def down(d):
+        return lax.rem(z + depth - d, depth)
+
+    xn, yn, partner = dev(z, y, 1 - x, core), dev(z, 1 - y, x, core), dev(z, y, x, 1 - core)
+    sent = []
+
+    def copy(src, dst, key, target):
+        i = keys[key]
+        return pltpu.make_async_remote_copy(
+            src_ref=src, dst_ref=dst, send_sem=send_sem.at[i], recv_sem=recv_sem.at[i],
+            device_id=(target,), device_id_type=MESH,
+        )
+
+    def send(src, dst, key, target):
+        c = copy(src, dst, key, target)
+        c.start()
+        sent.append(c)
+
+    def arrived(dst, key):
+        copy(dst, dst, key, partner).wait_recv()
+
+    barrier = pltpu.get_barrier_semaphore()
+    for d in range(1, n):
+        pl.semaphore_signal(barrier, inc=1, device_id=(lax.rem(me + d, n),), device_id_type=MESH)
+
+    t = jnp.exp(jnp.full((1, 1), lf_ref[0], F32))
+    bias = bias_ref[0]
+    text = t_ref[...].astype(F32)
+    text_length = jnp.sqrt(jnp.sum(text * text, axis=1, keepdims=True) + epsilon)
+    text_low[...] = (text / text_length).astype(BF)
+    w_all[me] = w_ref[...]
+
+    pl.semaphore_wait(barrier, n - 1)
+
+    send(w_ref.at[:, A], w_all.at[me, :, A], ("x1", 0), xn)
+    send(w_ref.at[:, B], w_all.at[me, :, B], ("y1", 0), yn)
+    for d in range(1, depth):
+        send(w_ref, w_all.at[me], ("z", d), dev(up(d), y, x, core))
+    send(w_ref.at[:, A], w_all.at[me, :, A], ("y3", 0, 0), yn)
+    send(w_ref.at[:, B], w_all.at[me, :, B], ("x3", 0, 0), xn)
+    send(w_ref, w_all.at[me], ("w", 0, 0), partner)
+
+    below, above = lax.rem(me + n - 2, n), lax.rem(me + 2, n)
+
+    def send_block(buf, slots, key, toward, far):
+        base = toward - core
+        for c in range(2):
+            part = pl.ds(c * half, half)
+            i = keys[(key, "in", 0)] + core
+            cp = pltpu.make_async_remote_copy(
+                src_ref=buf.at[part], dst_ref=slots.at[core, part],
+                send_sem=send_sem.at[keys[(key, "in", c)]], recv_sem=recv_sem.at[i],
+                device_id=(base + c,), device_id_type=MESH,
+            )
+            cp.start()
+            sent.append(cp)
+        send(buf, slots.at[2], (key, "far"), far)
+
+    def swap_block(slots, key):
+        part = pl.ds(pl.multiple_of(core * half, half), half)
+        for q in range(2):
+            arrived(slots.at[q, part], (key, "in", q))
+            send(slots.at[q, part], slots.at[q, part], (key, "on", q), partner)
+
+    def wait_block(slots, key, q):
+        part = pl.ds(pl.multiple_of((1 - core) * half, half), half)
+        arrived(slots.at[q, part], (key, "on", q))
+
+    send_block(text_low, text_in, "t", below, lax.rem(me + n - 3 + 2 * core, n))
+
+    xt[...] = x_ref[...].T
+
+    def step_z(d):
+        s = dev(down(d), y, x, core)
+        arrived(w_all.at[s], ("z", d))
+        send(w_all.at[s, :, A], w_all.at[s, :, A], ("x1", d), xn)
+        send(w_all.at[s, :, B], w_all.at[s, :, B], ("y1", d), yn)
+        send(w_all.at[s, :, A], w_all.at[s, :, A], ("y3", d, 0), yn)
+        send(w_all.at[s, :, B], w_all.at[s, :, B], ("x3", d, 0), xn)
+        send(w_all.at[s], w_all.at[s], ("w", d, 0), partner)
+
+    def step_one(d):
+        s = w_all.at[dev(down(d), y, 1 - x, core), :, A]
+        arrived(s, ("x1", d))
+        send(s, s, ("y3", d, 1), yn)
+        send(s, s, ("w", d, 1), partner)
+        s = w_all.at[dev(down(d), 1 - y, x, core), :, B]
+        arrived(s, ("y1", d))
+        send(s, s, ("x3", d, 1), xn)
+        send(s, s, ("w", d, 2), partner)
+
+    def step_two(d):
+        for i, x_ in enumerate((x, 1 - x)):
+            s = w_all.at[dev(down(d), 1 - y, x_, core), :, A]
+            arrived(s, ("y3", d, i))
+            send(s, s, ("w", d, 3 + i), partner)
+        for i, y_ in enumerate((y, 1 - y)):
+            s = w_all.at[dev(down(d), y_, 1 - x, core), :, B]
+            arrived(s, ("x3", d, i))
+            send(s, s, ("w", d, 5 + i), partner)
+
+    for step in range(depth + 2):
+        if 1 <= step < depth:
+            step_z(step)
+        if 0 <= step - 1 < depth:
+            step_one(step - 1)
+        if 0 <= step - 2 < depth:
+            step_two(step - 2)
+
+    other = 1 - core
+    for d in range(depth):
+        zs = down(d)
+        arrived(w_all.at[dev(zs, y, x, other)], ("w", d, 0))
+        arrived(w_all.at[dev(zs, y, 1 - x, other), :, A], ("w", d, 1))
+        arrived(w_all.at[dev(zs, 1 - y, x, other), :, B], ("w", d, 2))
+        for i, x_ in enumerate((x, 1 - x)):
+            arrived(w_all.at[dev(zs, 1 - y, x_, other), :, A], ("w", d, 3 + i))
+        for i, y_ in enumerate((y, 1 - y)):
+            arrived(w_all.at[dev(zs, y_, 1 - x, other), :, B], ("w", d, 5 + i))
+
+    weight = w_all[...].reshape(n * own_rows, cols)
+    embedded = jnp.dot(x_ref[...], weight, preferred_element_type=F32)
+    image_length = jnp.sqrt(jnp.sum(embedded * embedded, axis=1, keepdims=True) + epsilon)
+    image_unit = embedded / image_length
+    image_low[...] = image_unit.astype(BF)
+    mine = image_low[...]
+    own_text = text_low[...]
+
+    grad = pair_grad(mine, own_text, t, bias, True)
+    image_grad = jnp.dot(grad, own_text, preferred_element_type=F32)
+    send_block(image_low, image_in, "i", above, lax.rem(me + 1 + 2 * core, n))
+
+    swap_block(text_in, "t")
+    arrived(text_in.at[2], ("t", "far"))
+    for q in (2, 0, 1):
+        if q < 2:
+            wait_block(text_in, "t", q)
+        block = text_in[q]
+        image_grad += jnp.dot(
+            pair_grad(mine, block, t, bias, False), block, preferred_element_type=F32
+        )
+    along = jnp.sum(image_unit * image_grad, axis=1, keepdims=True)
+    embed_grad = ((image_grad - image_unit * along) / image_length).astype(BF)
+
+    order = [d for d in range(1, depth)] + [0]
+    group = 8 * own_rows
+    for d in order:
+        lhs = xt[pl.ds(pl.multiple_of(up(d) * group, group), group), :]
+        part = jnp.dot(lhs, embed_grad, preferred_element_type=F32)
+        gz[d] = part.reshape(4, 2, own_rows, cols)
+        for c in range(4):
+            to_core[d, c] = gz[d, c, other].astype(BF)
+        send(to_core.at[d], from_core.at[d], ("g0", d), partner)
+
+    def base(d, c, cut):
+        return gz[d, c, core, :, cut] + from_core[d, c, :, cut].astype(F32)
+
+    swap_block(image_in, "i")
+    gx_ref[...] = dot_nt(embed_grad, weight).astype(BF)
+
+    for d in order:
+        arrived(from_core.at[d], ("g0", d))
+        for i in range(2):
+            s1a[d, i] = base(d, (1 - y) * 2 + i, A).astype(BF)
+            s1b[d, i] = base(d, i * 2 + 1 - x, B).astype(BF)
+        send(s1a.at[d], r1a.at[d], ("g1a", d), yn)
+        send(s1b.at[d], r1b.at[d], ("g1b", d), xn)
+
+    text_grad = jnp.dot(
+        pair_grad(own_text, mine, t, bias, True), mine, preferred_element_type=F32
+    )
+
+    def stage_two(d):
+        arrived(r1a.at[d], ("g1a", d))
+        s2a[d] = (base(d, y * 2 + 1 - x, A) + r1a[d, 1 - x].astype(F32)).astype(BF)
+        send(s2a.at[d], r2a.at[d], ("g2a", d), xn)
+        arrived(r1b.at[d], ("g1b", d))
+        s2b[d] = (base(d, (1 - y) * 2 + x, B) + r1b[d, 1 - y].astype(F32)).astype(BF)
+        send(s2b.at[d], r2b.at[d], ("g2b", d), yn)
+
+    def stage_three(d):
+        here = y * 2 + x
+        arrived(r2a.at[d], ("g2a", d))
+        arrived(r2b.at[d], ("g2b", d))
+        left = base(d, here, A) + r1a[d, x].astype(F32) + r2a[d].astype(F32)
+        right = base(d, here, B) + r1b[d, y].astype(F32) + r2b[d].astype(F32)
+        if d == 0:
+            gw_ref[:, A] = left
+            gw_ref[:, B] = right
+        else:
+            s3[d, :, A] = left.astype(BF)
+            s3[d, :, B] = right.astype(BF)
+            send(s3.at[d], r3.at[d], ("g3", d), dev(up(d), y, x, core))
+
+    for i, d in enumerate(order):
+        stage_two(d)
+        if i >= 1:
+            stage_three(order[i - 1])
+
+    for q in (2, 0, 1):
+        if q < 2:
+            wait_block(image_in, "i", q)
+        else:
+            arrived(image_in.at[2], ("i", "far"))
+        block = image_in[q]
+        text_grad += jnp.dot(
+            pair_grad(own_text, block, t, bias, False), block, preferred_element_type=F32
+        )
+    text_unit = t_ref[...].astype(F32) / text_length
+    along = jnp.sum(text_unit * text_grad, axis=1, keepdims=True)
+    gt_ref[...] = ((text_grad - text_unit * along) / text_length).astype(BF)
+
+    stage_three(order[-1])
+    total = gw_ref[...]
+    for d in range(1, depth):
+        arrived(r3.at[d], ("g3", d))
+        total += r3[d].astype(F32)
+    gw_ref[...] = total
+    for c in sent:
+        c.wait_send()
+
+
+def fused(n, axis, image_features, head_weight, text_embeds, factor, bias):
+    depth = n // 8
+    rows, width = image_features.shape
+    own_rows, cols = head_weight.shape
+    keys = sem_keys(depth)
+    ha = (cols // 128 + 1) // 2 * 128
+    hb = cols - ha
+    vmem = pl.BlockSpec(memory_space=pltpu.VMEM)
+    smem = pl.BlockSpec(memory_space=pltpu.SMEM)
+    scratch = [
+        ((n, own_rows, cols), BF),
+        ((rows, cols), BF),
+        ((3, rows, cols), BF),
+        ((rows, cols), BF),
+        ((3, rows, cols), BF),
+        ((width, rows), BF),
+        ((depth, 4, 2, own_rows, cols), F32),
+        ((depth, 4, own_rows, cols), BF),
+        ((depth, 4, own_rows, cols), BF),
+        ((depth, 2, own_rows, ha), BF),
+        ((depth, 2, own_rows, hb), BF),
+        ((depth, 2, own_rows, ha), BF),
+        ((depth, 2, own_rows, hb), BF),
+        ((depth, own_rows, ha), BF),
+        ((depth, own_rows, hb), BF),
+        ((depth, own_rows, ha), BF),
+        ((depth, own_rows, hb), BF),
+        ((depth, own_rows, cols), BF),
+        ((depth, own_rows, cols), BF),
+    ]
+    return pl.pallas_call(
+        functools.partial(kernel, n, axis, keys),
+        out_shape=(
+            jax.ShapeDtypeStruct((rows, width), BF),
+            jax.ShapeDtypeStruct((rows, cols), BF),
+            jax.ShapeDtypeStruct((own_rows, cols), F32),
+        ),
+        in_specs=[vmem, vmem, vmem, smem, smem],
+        out_specs=(vmem, vmem, vmem),
+        scratch_shapes=[pltpu.VMEM(s, d) for s, d in scratch]
+        + [pltpu.SemaphoreType.DMA((len(keys),))] * 2,
+        compiler_params=pltpu.CompilerParams(
+            collective_id=0, has_side_effects=True, vmem_limit_bytes=60 * 2**20
+        ),
+    )(image_features, head_weight, text_embeds, factor, bias)
 
 
 def passed_along(block, axis, distance):
@@ -56,7 +383,7 @@
     return (grad - unit_rows * jnp.sum(unit_rows * grad, axis=1, keepdims=True)) / length
 
 
-def on_device(image_features, head_weight, text_embeds, natural_exponent_factor, logit_bias):
+def by_collectives(image_features, head_weight, text_embeds, natural_exponent_factor, logit_bias):
     full_weight = lax.all_gather(head_weight, "blk", axis=0, tiled=True)
     embedded = jnp.dot(image_features, full_weight, preferred_element_type=jnp.float32)
     image_unit, image_length = normalize(embedded)
@@ -107,6 +434,13 @@
     return (grad_features, grad_text, grad_weight)
 
 
+def on_device(image_features, head_weight, text_embeds, natural_exponent_factor, logit_bias):
+    n = lax.axis_size("blk")
+    whole_tiles = head_weight.shape[0] % 16 == 0 and n % 8 == 0 and n > 8
+    run = functools.partial(fused, n, "blk") if whole_tiles else by_collectives
+    return run(image_features, head_weight, text_embeds, natural_exponent_factor, logit_bias)
+
+
 def solution(mesh):
     return jax.shard_map(
         on_device,

time: 236 us -> 112 us (0.47)
  the two profiles are of different devices: /device:TPU:0 before, /device:TPU:18 now
where the time goes in v1:
time: 112 us
  Pallas kernels  106 us (95%)
  local copies, waits for them, and re-layouts  3.96 us (4%)
  between operations  1.94 us (2%)
    pallas_call x1, Pallas kernels, fused(): pl.pallas_call(functools.partial(kernel, n, axis, keys), out_shape=(jax.S...  106 us
    unnamed x7, local copies, waits for them, and re-layouts  3.96 us

profile of v1, /device:TPU:18, one launch (start us, length us, event | category | flops | bytes accessed | tf_op | source)
XLA Modules:
  0.0 111.9 jit_solution(3549084842813251413)
XLA Ops:
  1.9 106.0 %shard_map.76 = (bf16[256,1536]{1,0:T(8,128)(2,1)}, bf16[256,1152]{1,0:T(8,128)(2,1)}, f32[48,1152]{1,0:T(8,128)}) custom-call(bf16[256,1536]{1,0:T(8,128)(2,1)} %x_ref.1, bf16[48,1152]{1,0:T(8,128)(2,1)} %w_ref.1, bf16[256,1152]{1,0:T(8,128)(2,1)} %t_ref.1, f32[1]{0:T(128)S(6)} %copy.11.lf_ref, f32[1]{0:T(128)S(6)} %copy.12.bias_ref), custom_call_target="tpu_custom_call" | custom-call | tf_op jit(solution)/shard_map/pallas_call | solution.py:322
  108.0 0.0 copy-start
  108.0 2.1 %copy.13 = bf16[256,1536]{1,0:T(8,128)(2,1)} copy(bf16[256,1536]{1,0:T(8,128)(2,1)} %get-tuple-element.6) | data formatting | bytes 1572864
  110.1 0.0 copy-done
  110.1 0.0 copy-start.1
  110.1 0.8 copy.14
  110.9 0.3 copy-done.1
  111.3 0.7 copy.15
Async XLA Ops:
  108.0 2.1 %copy-start = (bf16[256,1152]{1,0:T(8,128)(2,1)S(1)}, bf16[256,1152]{1,0:T(8,128)(2,1)}, u32[]{:S(2)}) copy-start(bf16[256,1152]{1,0:T(8,128)(2,1)} %get-tuple-element.7) | copy-start | bytes 1769476
  110.1 1.1 %copy-start.1 = (f32[48,1152]{1,0:T(8,128)S(1)}, f32[48,1152]{1,0:T(8,128)}, u32[]{:S(2)}) copy-start(f32[48,1152]{1,0:T(8,128)} %get-tuple-element.8) | copy-start | bytes 663556

commit v2 on v1

--- a/solution.py
+++ b/solution.py
@@ -30,11 +30,11 @@
 
 
 def sem_keys(depth):
-    keys = [("z", d) for d in range(1, depth)]
+    keys = ["za", "zb", "g3a", "g3b"] + [("z", d) for d in range(1, depth)]
     for d in range(depth):
         keys += [("x1", d), ("y1", d), ("y3", d, 0), ("y3", d, 1), ("x3", d, 0), ("x3", d, 1)]
-        keys += [("w", d, i) for i in range(7)]
-        keys += [(k, d) for k in ("g0", "g1a", "g1b", "g2a", "g2b", "g3")]
+        keys += [("w", d, i) for i in range(8)]
+        keys += [(k, d) for k in ("g0", "g1a", "g1b", "g2a", "g2b")]
     for k in ("t", "i"):
         keys += [(k, "in", 0), (k, "in", 1), (k, "on", 0), (k, "on", 1), (k, "far")]
     return {k: i for i, k in enumerate(keys)}
@@ -45,10 +45,12 @@
     x_ref, w_ref, t_ref, lf_ref, bias_ref,
     gx_ref, gt_ref, gw_ref,
     w_all, text_low, text_in, image_low, image_in, xt, gz, from_core, to_core,
-    s1a, s1b, r1a, r1b, s2a, s2b, r2a, r2b, s3, r3,
+    s1a, s1b, r1a, r1b, s2a, s2b, r2a, r2b, s3a, s3b, r3a, r3b,
     send_sem, recv_sem,
 ):
     depth = n // 8
+    opp = depth // 2
+    near = [d for d in range(1, depth) if d != opp]
     rows, width = x_ref.shape
     own_rows, cols = w_ref.shape
     half = rows // 2
@@ -103,7 +105,7 @@
 
     send(w_ref.at[:, A], w_all.at[me, :, A], ("x1", 0), xn)
     send(w_ref.at[:, B], w_all.at[me, :, B], ("y1", 0), yn)
-    for d in range(1, depth):
+    for d in near:
         send(w_ref, w_all.at[me], ("z", d), dev(up(d), y, x, core))
     send(w_ref.at[:, A], w_all.at[me, :, A], ("y3", 0, 0), yn)
     send(w_ref.at[:, B], w_all.at[me, :, B], ("x3", 0, 0), xn)
@@ -135,26 +137,56 @@
         part = pl.ds(pl.multiple_of((1 - core) * half, half), half)
         arrived(slots.at[q, part], (key, "on", q))
 
-    send_block(text_low, text_in, "t", below, lax.rem(me + n - 3 + 2 * core, n))
 
     xt[...] = x_ref[...].T
+
+    def onward(part, d, key_a, key_b):
+        if key_a is not None and d == opp - 1:
+            send(part(A), part(A), key_a, dev(up(1), y, x, core))
+        if key_b is not None and d == opp + 1:
+            send(part(B), part(B), key_b, dev(down(1), y, x, core))
 
     def step_z(d):
         s = dev(down(d), y, x, core)
+
+        def part(cut):
+            return w_all.at[s, :, cut]
+
+        if d == opp:
+            arrived(part(A), "za")
+            send(part(A), part(A), ("y3", d, 0), yn)
+            send(part(A), part(A), ("w", d, 0), partner)
+            arrived(part(B), "zb")
+            send(part(B), part(B), ("x3", d, 0), xn)
+            send(part(B), part(B), ("w", d, 7), partner)
+            return
         arrived(w_all.at[s], ("z", d))
-        send(w_all.at[s, :, A], w_all.at[s, :, A], ("x1", d), xn)
-        send(w_all.at[s, :, B], w_all.at[s, :, B], ("y1", d), yn)
-        send(w_all.at[s, :, A], w_all.at[s, :, A], ("y3", d, 0), yn)
-        send(w_all.at[s, :, B], w_all.at[s, :, B], ("x3", d, 0), xn)
+        onward(part, d, "za", "zb")
+        send(part(A), part(A), ("y3", d, 0), yn)
+        send(part(B), part(B), ("x3", d, 0), xn)
         send(w_all.at[s], w_all.at[s], ("w", d, 0), partner)
 
     def step_one(d):
-        s = w_all.at[dev(down(d), y, 1 - x, core), :, A]
+        def side(cut):
+            return w_all.at[dev(down(d), y, 1 - x, core), :, cut]
+
+        def front(cut):
+            return w_all.at[dev(down(d), 1 - y, x, core), :, cut]
+
+        s = side(A)
         arrived(s, ("x1", d))
+        if d == 0:
+            for e in near:
+                send(s, s, ("x1", e), dev(up(e), y, x, core))
+        onward(side, d, ("x1", opp), None)
         send(s, s, ("y3", d, 1), yn)
         send(s, s, ("w", d, 1), partner)
-        s = w_all.at[dev(down(d), 1 - y, x, core), :, B]
+        s = front(B)
         arrived(s, ("y1", d))
+        if d == 0:
+            for e in near:
+                send(s, s, ("y1", e), dev(up(e), y, x, core))
+        onward(front, d, None, ("y1", opp))
         send(s, s, ("x3", d, 1), xn)
         send(s, s, ("w", d, 2), partner)
 
@@ -168,18 +200,25 @@
             arrived(s, ("x3", d, i))
             send(s, s, ("w", d, 5 + i), partner)
 
-    for step in range(depth + 2):
-        if 1 <= step < depth:
-            step_z(step)
-        if 0 <= step - 1 < depth:
-            step_one(step - 1)
-        if 0 <= step - 2 < depth:
-            step_two(step - 2)
-
+    step_one(0)
+    for d in near:
+        step_z(d)
+    for d in near:
+        step_one(d)
+    step_z(opp)
+    step_one(opp)
+    for d in [0] + near + [opp]:
+        step_two(d)
+
+    send_block(text_low, text_in, "t", below, lax.rem(me + n - 3 + 2 * core, n))
     other = 1 - core
     for d in range(depth):
         zs = down(d)
-        arrived(w_all.at[dev(zs, y, x, other)], ("w", d, 0))
+        if d == opp:
+            arrived(w_all.at[dev(zs, y, x, other), :, A], ("w", d, 0))
+            arrived(w_all.at[dev(zs, y, x, other), :, B], ("w", d, 7))
+        else:
+            arrived(w_all.at[dev(zs, y, x, other)], ("w", d, 0))
         arrived(w_all.at[dev(zs, y, 1 - x, other), :, A], ("w", d, 1))
         arrived(w_all.at[dev(zs, 1 - y, x, other), :, B], ("w", d, 2))
         for i, x_ in enumerate((x, 1 - x)):
@@ -211,7 +250,7 @@
     along = jnp.sum(image_unit * image_grad, axis=1, keepdims=True)
     embed_grad = ((image_grad - image_unit * along) / image_length).astype(BF)
 
-    order = [d for d in range(1, depth)] + [0]
+    order = [opp] + near + [0]
     group = 8 * own_rows
     for d in order:
         lhs = xt[pl.ds(pl.multiple_of(up(d) * group, group), group), :]
@@ -241,30 +280,34 @@
 
     def stage_two(d):
         arrived(r1a.at[d], ("g1a", d))
-        s2a[d] = (base(d, y * 2 + 1 - x, A) + r1a[d, 1 - x].astype(F32)).astype(BF)
-        send(s2a.at[d], r2a.at[d], ("g2a", d), xn)
         arrived(r1b.at[d], ("g1b", d))
-        s2b[d] = (base(d, (1 - y) * 2 + x, B) + r1b[d, 1 - y].astype(F32)).astype(BF)
-        send(s2b.at[d], r2b.at[d], ("g2b", d), yn)
-
-    def stage_three(d):
-        here = y * 2 + x
-        arrived(r2a.at[d], ("g2a", d))
-        arrived(r2b.at[d], ("g2b", d))
-        left = base(d, here, A) + r1a[d, x].astype(F32) + r2a[d].astype(F32)
-        right = base(d, here, B) + r1b[d, y].astype(F32) + r2b[d].astype(F32)
-        if d == 0:
-            gw_ref[:, A] = left
-            gw_ref[:, B] = right
-        else:
-            s3[d, :, A] = left.astype(BF)
-            s3[d, :, B] = right.astype(BF)
-            send(s3.at[d], r3.at[d], ("g3", d), dev(up(d), y, x, core))
-
-    for i, d in enumerate(order):
+        if d == opp - 1:
+            arrived(r2a.at[opp], ("g2a", opp))
+        if d == opp + 1:
+            arrived(r2b.at[opp], ("g2b", opp))
+        for i in range(2):
+            left = base(d, y * 2 + i, A) + r1a[d, i].astype(F32)
+            right = base(d, i * 2 + x, B) + r1b[d, i].astype(F32)
+            if d == opp - 1:
+                left += r2a[opp, i].astype(F32)
+            if d == opp + 1:
+                right += r2b[opp, i].astype(F32)
+            s2a[d, i] = left.astype(BF)
+            s2b[d, i] = right.astype(BF)
+        ta, tb = (up(1), down(1)) if d == opp else (up(d), up(d))
+        send(s2a.at[d], r2a.at[d], ("g2a", d), dev(ta, y, x, core))
+        send(s2b.at[d], r2b.at[d], ("g2b", d), dev(tb, y, x, core))
+
+    def gathered(i, j):
+        left = base(0, y * 2 + i, A) + r1a[0, i].astype(F32)
+        right = base(0, j * 2 + x, B) + r1b[0, j].astype(F32)
+        for d in near:
+            left += r2a[d, i].astype(F32)
+            right += r2b[d, j].astype(F32)
+        return left, right
+
+    for d in [opp] + near:
         stage_two(d)
-        if i >= 1:
-            stage_three(order[i - 1])
 
     for q in (2, 0, 1):
         if q < 2:
@@ -275,16 +318,27 @@
         text_grad += jnp.dot(
             pair_grad(own_text, block, t, bias, False), block, preferred_element_type=F32
         )
+    arrived(r1a.at[0], ("g1a", 0))
+    arrived(r1b.at[0], ("g1b", 0))
+    for d in near:
+        arrived(r2a.at[d], ("g2a", d))
+        arrived(r2b.at[d], ("g2b", d))
+    left, right = gathered(1 - x, 1 - y)
+    s3a[...] = left.astype(BF)
+    s3b[...] = right.astype(BF)
+    send(s3a, r3a, "g3a", xn)
+    send(s3b, r3b, "g3b", yn)
+    left, right = gathered(x, y)
+    gw_ref[:, A] = left
+    gw_ref[:, B] = right
     text_unit = t_ref[...].astype(F32) / text_length
     along = jnp.sum(text_unit * text_grad, axis=1, keepdims=True)
     gt_ref[...] = ((text_grad - text_unit * along) / text_length).astype(BF)
 
-    stage_three(order[-1])
-    total = gw_ref[...]
-    for d in range(1, depth):
-        arrived(r3.at[d], ("g3", d))
-        total += r3[d].astype(F32)
-    gw_ref[...] = total
+    arrived(r3a, "g3a")
+    arrived(r3b, "g3b")
+    gw_ref[:, A] += r3a[...].astype(F32)
+    gw_ref[:, B] += r3b[...].astype(F32)
     for c in sent:
         c.wait_send()
 
@@ -312,12 +366,14 @@
         ((depth, 2, own_rows, hb), BF),
         ((depth, 2, own_rows, ha), BF),
         ((depth, 2, own_rows, hb), BF),
-        ((depth, own_rows, ha), BF),
-        ((depth, own_rows, hb), BF),
-        ((depth, own_rows, ha), BF),
-        ((depth, own_rows, hb), BF),
-        ((depth, own_rows, cols), BF),
-        ((depth, own_rows, cols), BF),
+        ((depth, 2, own_rows, ha), BF),
+        ((depth, 2, own_rows, hb), BF),
+        ((depth, 2, own_rows, ha), BF),
+        ((depth, 2, own_rows, hb), BF),
+        ((own_rows, ha), BF),
+        ((own_rows, hb), BF),
+        ((own_rows, ha), BF),
+        ((own_rows, hb), BF),
     ]
     return pl.pallas_call(
         functools.partial(kernel, n, axis, keys),
@@ -436,7 +492,7 @@
 
 def on_device(image_features, head_weight, text_embeds, natural_exponent_factor, logit_bias):
     n = lax.axis_size("blk")
-    whole_tiles = head_weight.shape[0] % 16 == 0 and n % 8 == 0 and n > 8
+    whole_tiles = head_weight.shape[0] % 16 == 0 and n % 16 == 0 and n > 16
     run = functools.partial(fused, n, "blk") if whole_tiles else by_collectives
     return run(image_features, head_weight, text_embeds, natural_exponent_factor, logit_bias)
 

time: 112 us -> 95.8 us (0.86)
  the two profiles are of different devices: /device:TPU:18 before, /device:TPU:0 now
where the time goes in v2:
time: 95.8 us; the launch traced here: 95.6 us
  Pallas kernels  89.7 us (94%)
  local copies, waits for them, and re-layouts  3.96 us (4%)
  between operations  1.94 us (2%)
    pallas_call x1, Pallas kernels, fused(): pl.pallas_call(functools.partial(kernel, n, axis, keys), out_shape=(jax.S...  89.7 us
    unnamed x7, local copies, waits for them, and re-layouts  3.96 us

profile of v2, /device:TPU:0, one launch (start us, length us, event | category | flops | bytes accessed | tf_op | source)
XLA Modules:
  0.0 95.6 jit_solution(7539600554813898470)
XLA Ops:
  1.9 89.7 %shard_map.76 = (bf16[256,1536]{1,0:T(8,128)(2,1)}, bf16[256,1152]{1,0:T(8,128)(2,1)}, f32[48,1152]{1,0:T(8,128)}) custom-call(bf16[256,1536]{1,0:T(8,128)(2,1)} %x_ref.1, bf16[48,1152]{1,0:T(8,128)(2,1)} %w_ref.1, bf16[256,1152]{1,0:T(8,128)(2,1)} %t_ref.1, f32[1]{0:T(128)S(6)} %copy.11.lf_ref, f32[1]{0:T(128)S(6)} %copy.12.bias_ref), custom_call_target="tpu_custom_call" | custom-call | tf_op jit(solution)/shard_map/pallas_call | solution.py:378
  91.6 0.0 copy-start
  91.6 2.1 %copy.13 = bf16[256,1536]{1,0:T(8,128)(2,1)} copy(bf16[256,1536]{1,0:T(8,128)(2,1)} %get-tuple-element.6) | data formatting | bytes 1572864
  93.7 0.0 copy-done
  93.7 0.0 copy-start.1
  93.7 0.8 copy.14
  94.6 0.3 copy-done.1
  94.9 0.7 copy.15
Async XLA Ops:
  91.6 2.1 %copy-start = (bf16[256,1152]{1,0:T(8,128)(2,1)S(1)}, bf16[256,1152]{1,0:T(8,128)(2,1)}, u32[]{:S(2)}) copy-start(bf16[256,1152]{1,0:T(8,128)(2,1)} %get-tuple-element.7) | copy-start | bytes 1769476
  93.7 1.1 %copy-start.1 = (f32[48,1152]{1,0:T(8,128)S(1)}, f32[48,1152]{1,0:T(8,128)}, u32[]{:S(2)}) copy-start(f32[48,1152]{1,0:T(8,128)} %get-tuple-element.8) | copy-start | bytes 663556

commit v3 on v2

--- a/solution.py
+++ b/solution.py
@@ -36,7 +36,8 @@
         keys += [("w", d, i) for i in range(8)]
         keys += [(k, d) for k in ("g0", "g1a", "g1b", "g2a", "g2b")]
     for k in ("t", "i"):
-        keys += [(k, "in", 0), (k, "in", 1), (k, "on", 0), (k, "on", 1), (k, "far")]
+        keys += [(k, "in", 0), (k, "in", 1), (k, "on", 0), (k, "on", 1), (k, "far", 0), (k, "far", 1)]
+        keys += [(k, "relay", 0), (k, "relay", 1)]
     return {k: i for i, k in enumerate(keys)}
 
 
@@ -74,6 +75,7 @@
 
     xn, yn, partner = dev(z, y, 1 - x, core), dev(z, 1 - y, x, core), dev(z, y, x, 1 - core)
     sent = []
+    sent_if = []
 
     def copy(src, dst, key, target):
         i = keys[key]
@@ -91,8 +93,13 @@
         copy(dst, dst, key, partner).wait_recv()
 
     barrier = pltpu.get_barrier_semaphore()
-    for d in range(1, n):
-        pl.semaphore_signal(barrier, inc=1, device_id=(lax.rem(me + d, n),), device_id_type=MESH)
+    first = me - core
+    peers = [partner, xn, yn] + [dev(up(d), y, x, core) for d in range(1, depth)]
+    peers += [lax.rem(first + n - 2 + c, n) for c in range(2)]
+    peers += [lax.rem(first + 2 + c, n) for c in range(2)]
+    peers += [lax.rem(me + n - 3 + 6 * core, n)]
+    for peer in peers:
+        pl.semaphore_signal(barrier, inc=1, device_id=(peer,), device_id_type=MESH)
 
     t = jnp.exp(jnp.full((1, 1), lf_ref[0], F32))
     bias = bias_ref[0]
@@ -101,7 +108,7 @@
     text_low[...] = (text / text_length).astype(BF)
     w_all[me] = w_ref[...]
 
-    pl.semaphore_wait(barrier, n - 1)
+    pl.semaphore_wait(barrier, len(peers))
 
     send(w_ref.at[:, A], w_all.at[me, :, A], ("x1", 0), xn)
     send(w_ref.at[:, B], w_all.at[me, :, B], ("y1", 0), yn)
@@ -113,19 +120,27 @@
 
     below, above = lax.rem(me + n - 2, n), lax.rem(me + 2, n)
 
-    def send_block(buf, slots, key, toward, far):
-        base = toward - core
+    def halves(buf, slots, q, key, kind, base, cond, far=False):
         for c in range(2):
             part = pl.ds(c * half, half)
-            i = keys[(key, "in", 0)] + core
             cp = pltpu.make_async_remote_copy(
-                src_ref=buf.at[part], dst_ref=slots.at[core, part],
-                send_sem=send_sem.at[keys[(key, "in", c)]], recv_sem=recv_sem.at[i],
+                src_ref=buf.at[part], dst_ref=slots.at[q, part],
+                send_sem=send_sem.at[keys[(key, kind, c)]],
+                recv_sem=recv_sem.at[keys[(key, "in", 0)] + q],
                 device_id=(base + c,), device_id_type=MESH,
             )
-            cp.start()
-            sent.append(cp)
-        send(buf, slots.at[2], (key, "far"), far)
+            if far:
+                arrived(slots.at[2, part], (key, "far", c))
+            pl.when(cond)(cp.start)
+            sent_if.append((cond, cp))
+
+    def send_far(buf, slots, key, far):
+        for c in range(2):
+            part = pl.ds(c * half, half)
+            send(buf.at[part], slots.at[2, part], (key, "far", c), far)
+
+    def relay_far(slots, key, q, cond):
+        halves(slots.at[2], slots, q, key, "relay", xn - core, cond, True)
 
     def swap_block(slots, key):
         part = pl.ds(pl.multiple_of(core * half, half), half)
@@ -137,8 +152,6 @@
         part = pl.ds(pl.multiple_of((1 - core) * half, half), half)
         arrived(slots.at[q, part], (key, "on", q))
 
-
-    xt[...] = x_ref[...].T
 
     def onward(part, d, key_a, key_b):
         if key_a is not None and d == opp - 1:
@@ -200,17 +213,22 @@
             arrived(s, ("x3", d, i))
             send(s, s, ("w", d, 5 + i), partner)
 
+    send_far(text_low, text_in, "t", lax.rem(me + n - 3 + 2 * core, n))
     step_one(0)
     for d in near:
         step_z(d)
+    passed_on = jnp.logical_and(x == 0, core == 0)
+    halves(text_low, text_in, core, "t", "in", below - core, jnp.logical_not(passed_on))
     for d in near:
         step_one(d)
+    relay_far(text_in, "t", 0, jnp.logical_and(x == 0, core == 1))
     step_z(opp)
     step_one(opp)
     for d in [0] + near + [opp]:
         step_two(d)
 
-    send_block(text_low, text_in, "t", below, lax.rem(me + n - 3 + 2 * core, n))
+    xt[...] = x_ref[...].T
+
     other = 1 - core
     for d in range(depth):
         zs = down(d)
@@ -236,10 +254,11 @@
 
     grad = pair_grad(mine, own_text, t, bias, True)
     image_grad = jnp.dot(grad, own_text, preferred_element_type=F32)
-    send_block(image_low, image_in, "i", above, lax.rem(me + 1 + 2 * core, n))
+    send_far(image_low, image_in, "i", lax.rem(me + 1 + 2 * core, n))
+    passed_on = jnp.logical_and(x == 1, core == 1)
+    halves(image_low, image_in, core, "i", "in", above - core, jnp.logical_not(passed_on))
 
     swap_block(text_in, "t")
-    arrived(text_in.at[2], ("t", "far"))
     for q in (2, 0, 1):
         if q < 2:
             wait_block(text_in, "t", q)
@@ -263,7 +282,7 @@
     def base(d, c, cut):
         return gz[d, c, core, :, cut] + from_core[d, c, :, cut].astype(F32)
 
-    swap_block(image_in, "i")
+    relay_far(image_in, "i", 1, jnp.logical_and(x == 1, core == 0))
     gx_ref[...] = dot_nt(embed_grad, weight).astype(BF)
 
     for d in order:
@@ -306,14 +325,13 @@
             right += r2b[d, j].astype(F32)
         return left, right
 
+    swap_block(image_in, "i")
     for d in [opp] + near:
         stage_two(d)
 
     for q in (2, 0, 1):
         if q < 2:
             wait_block(image_in, "i", q)
-        else:
-            arrived(image_in.at[2], ("i", "far"))
         block = image_in[q]
         text_grad += jnp.dot(
             pair_grad(own_text, block, t, bias, False), block, preferred_element_type=F32
@@ -341,6 +359,8 @@
     gw_ref[:, B] += r3b[...].astype(F32)
     for c in sent:
         c.wait_send()
+    for cond, c in sent_if:
+        pl.when(cond)(c.wait_send)
 
 
 def fused(n, axis, image_features, head_weight, text_embeds, factor, bias):

time: 95.8 us -> 89.1 us (0.930)
  Pallas kernels: 89.7 us -> 82.9 us
    pallas_call x1, Pallas kernels: 89.7 us -> 82.9 us  [fused(): pl.pallas_call(functools.partial(kernel, n, axis, keys), out_shape=(jax.S...]
where the time goes in v3:
time: 89.1 us; the launch traced here: 88.8 us
  Pallas kernels  82.9 us (93%)
  local copies, waits for them, and re-layouts  3.96 us (4%)
  between operations  1.94 us (2%)
    pallas_call x1, Pallas kernels, fused(): pl.pallas_call(functools.partial(kernel, n, axis, keys), out_shape=(jax.S...  82.9 us
    unnamed x7, local copies, waits for them, and re-layouts  3.96 us

profile of v3, /device:TPU:0, one launch (start us, length us, event | category | flops | bytes accessed | tf_op | source)
XLA Modules:
  0.0 88.8 jit_solution(16618870980561034328)
XLA Ops:
  1.9 82.9 %shard_map.76 = (bf16[256,1536]{1,0:T(8,128)(2,1)}, bf16[256,1152]{1,0:T(8,128)(2,1)}, f32[48,1152]{1,0:T(8,128)}) custom-call(bf16[256,1536]{1,0:T(8,128)(2,1)} %x_ref.1, bf16[48,1152]{1,0:T(8,128)(2,1)} %w_ref.1, bf16[256,1152]{1,0:T(8,128)(2,1)} %t_ref.1, f32[1]{0:T(128)S(6)} %copy.11.lf_ref, f32[1]{0:T(128)S(6)} %copy.12.bias_ref), custom_call_target="tpu_custom_call" | custom-call | tf_op jit(solution)/shard_map/pallas_call | solution.py:398
  84.9 0.0 copy-start
  84.9 2.1 %copy.13 = bf16[256,1536]{1,0:T(8,128)(2,1)} copy(bf16[256,1536]{1,0:T(8,128)(2,1)} %get-tuple-element.6) | data formatting | bytes 1572864
  87.0 0.0 copy-done
  87.0 0.0 copy-start.1
  87.0 0.8 copy.14
  87.8 0.3 copy-done.1
  88.2 0.7 copy.15
Async XLA Ops:
  84.9 2.1 %copy-start = (bf16[256,1152]{1,0:T(8,128)(2,1)S(1)}, bf16[256,1152]{1,0:T(8,128)(2,1)}, u32[]{:S(2)}) copy-start(bf16[256,1152]{1,0:T(8,128)(2,1)} %get-tuple-element.7) | copy-start | bytes 1769476
  87.0 1.1 %copy-start.1 = (f32[48,1152]{1,0:T(8,128)S(1)}, f32[48,1152]{1,0:T(8,128)}, u32[]{:S(2)}) copy-start(f32[48,1152]{1,0:T(8,128)} %get-tuple-element.8) | copy-start | bytes 663556
